TPU v7x, 32 devices: a whole 2x2x4 slice. The times are simulated.
32 devices in a mesh: node: 16 (over z, y, core), harm: 2 (over x).
Axes of the slice: x: 2, y: 2, z: 4, core: 2. Of those that a mesh axis runs over, the one named last changes fastest.
Arguments:
- spectrum: float32 [128, 3, 98304], P('harm', None, 'node'), may hold values from -2 to 2
- source: float32 [128, 3, 98304], P('harm', None, 'node'), may hold values from -4 to 4
- coupling: bfloat16 [768, 4, 128, 128], P('node'), may hold values from -0.75 to 0.75
- capacitance: float32 [98304], P('node'), may hold values from 0.5 to 4
- saturation: float32 [98304], P('node'), may hold values from 0.1 to 1
- steepness: float32 [98304], P('node'), may hold values from 0.5 to 4
- junction: float32 [98304], P('node'), may hold values from 0.2 to 2
- halo_list: int32 [16, 4, 4], replicated, may hold values from 0 to 47, as said below
- neighbour_slot: int32 [768, 4], P('node'), may hold values from 0 to 64, as said below
Outputs:
- residual: float32 [128, 3, 98304], P('harm', None, 'node')
Inputs may be any that keep to these rules, and one draw needn't show every extreme that they name: `halo_list`: row [m, j] lists 4 distinct blocks of device m, by index among its 48 blocks, needed by the device at index m + o_j along node, o = (-2, -1, 1, 2). `neighbour_slot`: column 0 of block b is b's own index among the 48 blocks of its device d. Other entries v: own block v if v < 48; block halo_list[m, j, s] of device m = d - o_j if v = 48 + j * 4 + s, only where m lies on the mesh; v = 64 is an empty entry. Every such slot of a device whose sender lies on the mesh is named by some entry of the device.
All inputs are finite; a program needn't handle non-finite values.
Results may differ from a plain program's by a relative error of at most 0.0025.
Values may be sent and summed in bfloat16 or wider, within the bound.
A program may use at most 128 MiB of HBM per device.

v0:
```python
import functools

import jax
import jax.numpy as jnp
import numpy as np
from jax import lax
from jax.experimental import pallas as pl
from jax.experimental.pallas import tpu as pltpu
from jax.sharding import PartitionSpec as P

LOG_TWO = 0.6931471805599453
OFFSETS = (-2, -1, 1, 2)
LANES = 128
VMEM_BYTES = 36 << 20
MESH = pl.DeviceIdType.MESH


def fourier_tables(length, shares):
    rows = length // shares
    sample = np.arange(length)[:, None]
    column = np.arange(length)[None, :]
    angle = 2.0 * np.pi / length * (column // 2 * sample % length)
    table = np.where(column % 2 == 1, np.sin(angle), np.cos(angle))
    table = np.where(column == 1, np.where(sample % 2 == 0, 1.0, -1.0), table)
    weights = np.where(np.arange(length) < 2, 1.0, 2.0) / length
    analysis = table.T * weights[:, None]
    pulsation = np.arange(length // 2)[:, None, None] / (length // 2)
    pairs = analysis.reshape(length // 2, 2, length)
    slope = np.concatenate([pulsation * pairs[:, 1:], -pulsation * pairs[:, :1]], axis=1)
    both = np.concatenate([analysis, slope.reshape(length, length)], axis=1)
    table = table.astype(np.float32)
    high = table.astype(jnp.bfloat16)
    low = (table - high.astype(np.float32)).astype(jnp.bfloat16)
    order = [
        np.concatenate([np.arange(rows) + (me - by) % shares * rows for by in range(shares)])
        for me in range(shares)
    ]
    synthesis = np.stack([np.concatenate([high[:, o], low[:, o]], axis=1) for o in order])
    return synthesis, both.astype(jnp.bfloat16).reshape(shares, rows, 2 * length)


def kernel(
    unit,
    list_ref,
    slot_ref,
    x_hbm,
    source_hbm,
    coupling_hbm,
    synthesis_hbm,
    analysis_hbm,
    capacitance_hbm,
    saturation_hbm,
    steepness_hbm,
    junction_hbm,
    out_ref,
    x_ref,
    coupling_ref,
    synthesis_ref,
    analysis_ref,
    scale_ref,
    pool_ref,
    arrived_ref,
    packed_ref,
    halo_ref,
    x_sem,
    local_sem,
    send_sem,
    recv_sem,
    halo_send_sem,
    halo_recv_sem,
):
    points, rows, nodes = x_ref.shape
    blocks = nodes // LANES
    width = unit * LANES
    chunks = blocks // unit
    count, slots = coupling_ref.shape[1], list_ref.shape[1]
    shares, devices = lax.axis_size("harm"), lax.axis_size("node")
    me, place = lax.axis_index("harm"), lax.axis_index("node")
    length = rows * shares

    def on_mesh(device):
        return jnp.logical_and(device >= 0, device < devices)

    def columns(chunk):
        return pl.ds(pl.multiple_of(chunk * width, width), width)

    def load(chunk):
        span = columns(chunk)
        return pltpu.make_async_copy(
            x_hbm.at[:, :, span], x_ref.at[:, :, span], x_sem.at[chunk]
        )

    def exchange(chunk, by):
        part = pl.ds(chunk * unit, unit)
        return pltpu.make_async_remote_copy(
            src_ref=pool_ref.at[part],
            dst_ref=arrived_ref.at[by - 1, part],
            send_sem=send_sem.at[by - 1, chunk],
            recv_sem=recv_sem.at[by - 1, chunk],
            device_id={"harm": lax.rem(me + by, shares)},
            device_id_type=MESH,
        )

    def halo(direction, device):
        return pltpu.make_async_remote_copy(
            src_ref=packed_ref.at[direction],
            dst_ref=halo_ref.at[direction],
            send_sem=halo_send_sem.at[direction],
            recv_sem=halo_recv_sem.at[direction],
            device_id={"node": device},
            device_id_type=MESH,
        )

    barrier = pltpu.get_barrier_semaphore()
    for by in range(1, shares):
        pl.semaphore_signal(
            barrier, inc=1, device_id={"harm": lax.rem(me + by, shares)}, device_id_type=MESH
        )
    greeted = shares - 1
    for offset in OFFSETS:
        there = on_mesh(place + offset)
        greeted = greeted + there.astype(jnp.int32)

        @pl.when(there)
        def _():
            pl.semaphore_signal(
                barrier, inc=1, device_id={"node": place + offset}, device_id_type=MESH
            )

    def start_load(chunk, carry):
        load(chunk).start()
        return carry

    lax.fori_loop(0, chunks, start_load, 0)
    local = [
        pltpu.make_async_copy(source, target, local_sem.at[i])
        for i, (source, target) in enumerate(
            [
                (source_hbm, out_ref),
                (coupling_hbm, coupling_ref),
                (capacitance_hbm, scale_ref.at[0]),
                (saturation_hbm, scale_ref.at[1]),
                (steepness_hbm, scale_ref.at[2]),
                (junction_hbm, scale_ref.at[3]),
                (synthesis_hbm.at[me], synthesis_ref),
                (analysis_hbm.at[me], analysis_ref),
            ]
        )
    ]
    for copy in local:
        copy.start()

    def round_chunk(chunk):
        load(chunk).wait()
        for inner in range(unit):
            block = chunk * unit + inner
            span = pl.ds(pl.multiple_of(block * LANES, LANES), LANES)
            for point in range(points):
                pool_ref[block, point * rows : (point + 1) * rows, :] = x_ref[
                    point, :, span
                ].astype(jnp.bfloat16)

    def send(chunk):
        for by in range(1, shares):
            exchange(chunk, by).start()

    round_chunk(0)
    pl.semaphore_wait(barrier, greeted)

    def advance(chunk, carry):
        round_chunk(chunk)
        send(chunk - 1)
        return carry

    lax.fori_loop(1, chunks, advance, 0)
    for direction in range(len(OFFSETS)):
        for slot in range(slots):
            packed_ref[direction, slot] = pool_ref[list_ref[direction, slot, place]]
    send(chunks - 1)
    for direction, offset in enumerate(OFFSETS):

        @pl.when(on_mesh(place + offset))
        def _():
            halo(direction, place + offset).start()

    pool_ref[blocks + len(OFFSETS) * slots] = jnp.zeros(pool_ref.shape[1:], pool_ref.dtype)
    for copy in local:
        copy.wait()
    for direction, offset in enumerate(OFFSETS):
        first = blocks + direction * slots
        there = on_mesh(place - offset)

        @pl.when(there)
        def _():
            halo(direction, place - offset).wait_recv()
            for slot in range(slots):
                pool_ref[first + slot] = halo_ref[direction, slot]

        @pl.when(jnp.logical_not(there))
        def _():
            for slot in range(slots):
                pool_ref[first + slot] = jnp.zeros(pool_ref.shape[1:], pool_ref.dtype)

    row = me * rows + lax.broadcasted_iota(jnp.int32, (rows, LANES), 0)
    even = row % 2 == 0
    rate = (row // 2).astype(jnp.float32) * (2.0 / length)
    rate = jnp.where(even, rate, -rate)

    def couple(block, carry):
        gathered = jnp.concatenate([pool_ref[slot_ref[k, block]] for k in range(count)], axis=1)
        matrix = jnp.concatenate([coupling_ref[block, k] for k in range(count)], axis=1)
        coupled = lax.dot_general(
            gathered, matrix, (((1,), (1,)), ((), ())), preferred_element_type=jnp.float32
        )
        scaled = rate * scale_ref[0, pl.ds(block, 1), :]
        span = pl.ds(pl.multiple_of(block * LANES, LANES), LANES)
        for point in range(points):
            values = x_ref[point, :, span]
            other = jnp.where(even, pltpu.roll(values, rows - 1, 0), pltpu.roll(values, 1, 0))
            out_ref[point, :, span] = (
                coupled[point * rows : (point + 1) * rows]
                + scaled * other
                - out_ref[point, :, span]
            )
        return carry

    lax.fori_loop(0, blocks, couple, 0, unroll=unit)

    def nonlinear(chunk, carry):
        for by in range(1, shares):
            exchange(chunk, by).wait_recv()
        ids = [chunk * unit + inner for inner in range(unit)]

        def scale(index):
            parts = [scale_ref[index, pl.ds(block, 1), :] for block in ids]
            return jnp.concatenate(parts, axis=1)

        saturation, steepness, junction = scale(1), scale(2), scale(3)
        span = columns(chunk)
        for point in range(points):
            held = slice(point * rows, (point + 1) * rows)
            spectra = [jnp.concatenate([pool_ref[block, held, :] for block in ids], axis=1)]
            for by in range(1, shares):
                spectra.append(
                    jnp.concatenate([arrived_ref[by - 1, block, held, :] for block in ids], axis=1)
                )
            stacked = jnp.concatenate(spectra + spectra, axis=0)
            voltage = jnp.dot(synthesis_ref[...], stacked, preferred_element_type=jnp.float32)
            drive = steepness * voltage
            softplus = jnp.maximum(drive, 0.0) + jnp.log(1.0 + jnp.exp(-jnp.abs(drive)))
            current = (saturation * (softplus - LOG_TWO)).astype(jnp.bfloat16)
            charge = (junction * voltage * lax.rsqrt(1.0 + voltage * voltage)).astype(jnp.bfloat16)
            samples = jnp.concatenate([current, charge], axis=0)
            out_ref[point, :, span] += jnp.dot(
                analysis_ref[...], samples, preferred_element_type=jnp.float32
            )
        return carry

    lax.fori_loop(0, chunks, nonlinear, 0)

    def drain(chunk, carry):
        for by in range(1, shares):
            exchange(chunk, by).wait_send()
        return carry

    lax.fori_loop(0, chunks, drain, 0)
    for direction, offset in enumerate(OFFSETS):

        @pl.when(on_mesh(place + offset))
        def _():
            halo(direction, place + offset).wait_send()


def local_part(
    spectrum,
    source,
    coupling,
    capacitance,
    saturation,
    steepness,
    junction,
    halo_list,
    neighbour_slot,
):
    rows, points, nodes = spectrum.shape
    shares = lax.axis_size("harm")
    length = rows * shares
    blocks = nodes // LANES
    unit = 2 if blocks % 2 == 0 else 1
    chunks = blocks // unit
    slots, count = halo_list.shape[2], neighbour_slot.shape[1]
    directions = len(OFFSETS)
    height = points * rows
    x = jnp.transpose(spectrum, (1, 0, 2))
    injected = jnp.transpose(source, (1, 0, 2))
    synthesis, analysis = (jnp.asarray(t) for t in fourier_tables(length, shares))
    scales = [v.reshape(blocks, LANES) for v in (capacitance, saturation, steepness, junction)]
    smem = pl.BlockSpec(memory_space=pltpu.SMEM)
    hbm = pl.BlockSpec(memory_space=pltpu.HBM)
    bf16, f32 = jnp.bfloat16, jnp.float32
    total = pl.pallas_call(
        functools.partial(kernel, unit),
        in_specs=[smem, smem] + [hbm] * 9,
        out_specs=pl.BlockSpec(memory_space=pltpu.VMEM),
        out_shape=pltpu.VMEM((points, rows, nodes), f32),
        scratch_shapes=[
            pltpu.VMEM((points, rows, nodes), f32),
            pltpu.VMEM((blocks, count, LANES, LANES), bf16),
            pltpu.VMEM((length, 2 * length), bf16),
            pltpu.VMEM((rows, 2 * length), bf16),
            pltpu.VMEM((4, blocks, LANES), f32),
            pltpu.VMEM((blocks + directions * slots + 1, height, LANES), bf16),
            pltpu.VMEM((shares - 1, blocks, height, LANES), bf16),
            pltpu.VMEM((directions, slots, height, LANES), bf16),
            pltpu.VMEM((directions, slots, height, LANES), bf16),
            pltpu.SemaphoreType.DMA((chunks,)),
            pltpu.SemaphoreType.DMA((8,)),
            pltpu.SemaphoreType.DMA((shares - 1, chunks)),
            pltpu.SemaphoreType.DMA((shares - 1, chunks)),
            pltpu.SemaphoreType.DMA((directions,)),
            pltpu.SemaphoreType.DMA((directions,)),
        ],
        compiler_params=pltpu.CompilerParams(
            collective_id=0, has_side_effects=True, vmem_limit_bytes=VMEM_BYTES
        ),
        cost_estimate=pl.CostEstimate(
            flops=2 * height * nodes * (count * LANES + 3 * length),
            bytes_accessed=coupling.size * 2 + 3 * x.size * 4,
            transcendentals=0,
        ),
        name="residual",
    )(
        jnp.transpose(halo_list, (1, 2, 0)),
        neighbour_slot.T,
        x,
        injected,
        coupling,
        synthesis,
        analysis,
        *scales,
    )
    return jnp.transpose(total, (1, 0, 2))


def solution(mesh):
    in_specs = (
        P("harm", None, "node"),
        P("harm", None, "node"),
        P("node", None, None, None),
        P("node"),
        P("node"),
        P("node"),
        P("node"),
        P(),
        P("node", None),
    )
    return jax.shard_map(
        local_part, mesh=mesh, in_specs=in_specs, out_specs=P("harm", None, "node"), check_vma=False
    )
```

profile of v0, /device:TPU:0, one launch (start us, length us, event | category | flops | bytes accessed | tf_op | source)
XLA Modules:
  0.0 71.2 jit_solution(10070098942120483862)
XLA Ops:
  0.0 0.0 copy-start
  0.0 2.3 %copy-done = f32[64,3,6144]{2,0,1:T(8,128)S(1)} copy-done((f32[64,3,6144]{2,0,1:T(8,128)S(1)}, f32[64,3,6144]{2,0,1:T(8,128)}, u32[]{:S(2)}) %copy-start) | copy-done | bytes 4718616
  2.3 0.0 copy-start.1
  2.3 2.3 %copy-done.1 = f32[64,3,6144]{2,0,1:T(8,128)S(1)} copy-done((f32[64,3,6144]{2,0,1:T(8,128)S(1)}, f32[64,3,6144]{2,0,1:T(8,128)}, u32[]{:S(2)}) %copy-start.1) | copy-done | bytes 4718616
  4.7 0.0 copy-start.2
  4.7 0.9 %copy-done.2 = bf16[2,128,256]{2,1,0:T(8,128)(2,1)S(1)} copy-done((bf16[2,128,256]{2,1,0:T(8,128)(2,1)S(1)}, bf16[2,128,256]{2,1,0:T(8,128)(2,1)}, u32[]{:S(2)}) %copy-start.2) | copy-done | bytes 131096
  5.6 0.0 copy-start.3
  5.6 0.8 %copy-done.3 = bf16[2,64,256]{2,1,0:T(8,128)(2,1)S(1)} copy-done((bf16[2,64,256]{2,1,0:T(8,128)(2,1)S(1)}, bf16[2,64,256]{2,1,0:T(8,128)(2,1)}, u32[]{:S(2)}) %copy-start.3) | copy-done | bytes 65560
  6.4 0.0 copy-start.4
  6.4 0.7 %copy-done.4 = f32[6144]{0:T(1024)S(1)} copy-done((f32[6144]{0:T(1024)S(1)}, f32[6144]{0:T(1024)}, u32[]{:S(2)}) %copy-start.4) | copy-done | bytes 24600
  7.2 0.0 copy-start.5
  7.2 0.7 %copy-done.5 = f32[6144]{0:T(1024)S(1)} copy-done((f32[6144]{0:T(1024)S(1)}, f32[6144]{0:T(1024)}, u32[]{:S(2)}) %copy-start.5) | copy-done | bytes 24600
  7.9 0.0 copy-start.6
  7.9 0.7 %copy-done.6 = f32[6144]{0:T(1024)S(1)} copy-done((f32[6144]{0:T(1024)S(1)}, f32[6144]{0:T(1024)}, u32[]{:S(2)}) %copy-start.6) | copy-done | bytes 24600
  8.6 0.0 copy-start.7
  8.6 0.7 %copy-done.7 = f32[6144]{0:T(1024)S(1)} copy-done((f32[6144]{0:T(1024)S(1)}, f32[6144]{0:T(1024)}, u32[]{:S(2)}) %copy-start.7) | copy-done | bytes 24600
  9.4 0.0 copy-start.8
  9.4 0.7 copy-done.8
  10.1 0.0 copy-start.9
  10.1 0.7 copy-done.9
  10.8 58.2 %residual.1 = f32[3,64,6144]{2,1,0:T(8,128)S(1)} custom-call(s32[4,4,16]{2,1,0:T(4,128)S(1)} %bitcast.16, s32[4,48]{1,0:T(4,128)S(1)} %bitcast.17, f32[3,64,6144]{2,1,0:T(8,128)S(1)} %bitcast.10, f32[3,64,6144]{2,1,0:T(8,128)S(1)} %bitcast.11, bf16[48,4,128,128]{3,2,1,0:T(8,128)(2,1)} %coupling_hbm.1, bf16[2,128,256]{2,1,0:T(8,128)(2,1)S(1)} %copy-done.2, ...), custom_call_target="tpu_custom_call" | custom-call | flops 2113929216 | bytes 20447232 | tf_op jit(solution)/shard_map/residual/pallas_call | solution.py:301
  69.0 2.2 %copy.13 = f32[64,3,6144]{2,0,1:T(8,128)} copy(f32[64,3,6144]{2,0,1:T(8,128)S(1)} %bitcast.9) | data formatting | bytes 9437184
Async XLA Ops:
  0.0 2.3 %copy-start = (f32[64,3,6144]{2,0,1:T(8,128)S(1)}, f32[64,3,6144]{2,0,1:T(8,128)}, u32[]{:S(2)}) copy-start(f32[64,3,6144]{2,0,1:T(8,128)} %param.11) | copy-start | bytes 14155780
  2.3 2.3 %copy-start.1 = (f32[64,3,6144]{2,0,1:T(8,128)S(1)}, f32[64,3,6144]{2,0,1:T(8,128)}, u32[]{:S(2)}) copy-start(f32[64,3,6144]{2,0,1:T(8,128)} %param.12) | copy-start | bytes 14155780
  4.7 0.9 %copy-start.2 = (bf16[2,128,256]{2,1,0:T(8,128)(2,1)S(1)}, bf16[2,128,256]{2,1,0:T(8,128)(2,1)}, u32[]{:S(2)}) copy-start(bf16[2,128,256]{2,1,0:T(8,128)(2,1)} %constant.4.clone.synthesis_hbm) | copy-start | bytes 393220
  5.6 0.8 %copy-start.3 = (bf16[2,64,256]{2,1,0:T(8,128)(2,1)S(1)}, bf16[2,64,256]{2,1,0:T(8,128)(2,1)}, u32[]{:S(2)}) copy-start(bf16[2,64,256]{2,1,0:T(8,128)(2,1)} %constant.5.clone.analysis_hbm) | copy-start | bytes 196612
  6.4 0.7 %copy-start.4 = (f32[6144]{0:T(1024)S(1)}, f32[6144]{0:T(1024)}, u32[]{:S(2)}) copy-start(f32[6144]{0:T(1024)} %param.14) | copy-start | bytes 73732
  7.2 0.7 %copy-start.5 = (f32[6144]{0:T(1024)S(1)}, f32[6144]{0:T(1024)}, u32[]{:S(2)}) copy-start(f32[6144]{0:T(1024)} %param.15) | copy-start | bytes 73732
  7.9 0.7 %copy-start.6 = (f32[6144]{0:T(1024)S(1)}, f32[6144]{0:T(1024)}, u32[]{:S(2)}) copy-start(f32[6144]{0:T(1024)} %param.16) | copy-start | bytes 73732
  8.6 0.7 %copy-start.7 = (f32[6144]{0:T(1024)S(1)}, f32[6144]{0:T(1024)}, u32[]{:S(2)}) copy-start(f32[6144]{0:T(1024)} %param.17) | copy-start | bytes 73732
  9.4 0.7 copy-start.8
  10.1 0.7 copy-start.9
where the time goes:
time: 71.8 us; the launch traced here: 71.2 us
  Pallas kernels  58.2 us (81%)
  local copies, waits for them, and re-layouts  12.9 us (18%)
    pallas_call x1, Pallas kernels, local_part(): pl.pallas_call(functools.partial(kernel, unit), in_specs=[smem, smem] + [...  58.2 us
    unnamed x21, local copies, waits for them, and re-layouts  12.9 us

commit v1 on v0

--- a/solution.py
+++ b/solution.py
@@ -39,10 +39,59 @@
     return synthesis, both.astype(jnp.bfloat16).reshape(shares, rows, 2 * length)
 
 
+def evaluate(spectra, synthesis, analysis, saturation, steepness, junction):
+    stacked = jnp.concatenate(spectra + spectra, axis=0)
+    voltage = jnp.dot(synthesis, stacked, preferred_element_type=jnp.float32)
+    drive = steepness * voltage
+    softplus = jnp.maximum(drive, 0.0) + jnp.log(1.0 + jnp.exp(-jnp.abs(drive)))
+    current = (saturation * (softplus - LOG_TWO)).astype(jnp.bfloat16)
+    charge = (junction * voltage * lax.rsqrt(1.0 + voltage * voltage)).astype(jnp.bfloat16)
+    samples = jnp.concatenate([current, charge], axis=0)
+    return jnp.dot(analysis, samples, preferred_element_type=jnp.float32)
+
+
+def widen(scale_ref, index, blocks):
+    parts = [scale_ref[index, pl.ds(block, 1), :] for block in blocks]
+    return jnp.concatenate(parts, axis=1)
+
+
+def finish_kernel(pieces, total_ref, tail_ref, synthesis_ref, analysis_ref, scale_ref, out_hbm, last_ref, sem):
+    points, rows, nodes = total_ref.shape
+    shares, unit = tail_ref.shape[:2]
+    blocks = nodes // LANES
+    done = nodes - unit * LANES
+    copies = []
+    for point in range(points):
+        for piece in range(pieces):
+            part = (point, slice(piece * rows // pieces, (piece + 1) * rows // pieces), slice(0, done))
+            copies.append(
+                pltpu.make_async_copy(
+                    total_ref.at[part], out_hbm.at[part], sem.at[point * pieces + piece]
+                )
+            )
+    for copy in copies:
+        copy.start()
+    ids = range(blocks - unit, blocks)
+    scales = [widen(scale_ref, index, ids) for index in (1, 2, 3)]
+    for point in range(points):
+        held = slice(point * rows, (point + 1) * rows)
+        spectra = [
+            jnp.concatenate([tail_ref[share, inner, held, :] for inner in range(unit)], axis=1)
+            for share in range(shares)
+        ]
+        last_ref[point] = total_ref[point, :, done:] + evaluate(
+            spectra, synthesis_ref[...], analysis_ref[...], *scales
+        )
+    copy = pltpu.make_async_copy(last_ref, out_hbm.at[:, :, done:], sem.at[points * pieces])
+    copy.start()
+    for each in copies + [copy]:
+        each.wait()
+
+
 def kernel(
     unit,
-    list_ref,
-    slot_ref,
+    list_hbm,
+    slot_hbm,
     x_hbm,
     source_hbm,
     coupling_hbm,
@@ -53,11 +102,14 @@
     steepness_hbm,
     junction_hbm,
     out_ref,
-    x_ref,
-    coupling_ref,
+    tail_ref,
     synthesis_ref,
     analysis_ref,
     scale_ref,
+    list_ref,
+    slot_ref,
+    x_ref,
+    coupling_ref,
     pool_ref,
     arrived_ref,
     packed_ref,
@@ -136,6 +188,8 @@
         pltpu.make_async_copy(source, target, local_sem.at[i])
         for i, (source, target) in enumerate(
             [
+                (list_hbm, list_ref),
+                (slot_hbm, slot_ref),
                 (source_hbm, out_ref),
                 (coupling_hbm, coupling_ref),
                 (capacitance_hbm, scale_ref.at[0]),
@@ -147,8 +201,8 @@
             ]
         )
     ]
-    for copy in local:
-        copy.start()
+    local[0].start()
+    local[1].start()
 
     def round_chunk(chunk):
         load(chunk).wait()
@@ -165,6 +219,8 @@
             exchange(chunk, by).start()
 
     round_chunk(0)
+    for copy in local[2:]:
+        copy.start()
     pl.semaphore_wait(barrier, greeted)
 
     def advance(chunk, carry):
@@ -173,6 +229,8 @@
         return carry
 
     lax.fori_loop(1, chunks, advance, 0)
+    local[0].wait()
+    local[1].wait()
     for direction in range(len(OFFSETS)):
         for slot in range(slots):
             packed_ref[direction, slot] = pool_ref[list_ref[direction, slot, place]]
@@ -184,7 +242,7 @@
             halo(direction, place + offset).start()
 
     pool_ref[blocks + len(OFFSETS) * slots] = jnp.zeros(pool_ref.shape[1:], pool_ref.dtype)
-    for copy in local:
+    for copy in local[2:]:
         copy.wait()
     for direction, offset in enumerate(OFFSETS):
         first = blocks + direction * slots
@@ -230,12 +288,7 @@
         for by in range(1, shares):
             exchange(chunk, by).wait_recv()
         ids = [chunk * unit + inner for inner in range(unit)]
-
-        def scale(index):
-            parts = [scale_ref[index, pl.ds(block, 1), :] for block in ids]
-            return jnp.concatenate(parts, axis=1)
-
-        saturation, steepness, junction = scale(1), scale(2), scale(3)
+        scales = [widen(scale_ref, index, ids) for index in (1, 2, 3)]
         span = columns(chunk)
         for point in range(points):
             held = slice(point * rows, (point + 1) * rows)
@@ -244,19 +297,17 @@
                 spectra.append(
                     jnp.concatenate([arrived_ref[by - 1, block, held, :] for block in ids], axis=1)
                 )
-            stacked = jnp.concatenate(spectra + spectra, axis=0)
-            voltage = jnp.dot(synthesis_ref[...], stacked, preferred_element_type=jnp.float32)
-            drive = steepness * voltage
-            softplus = jnp.maximum(drive, 0.0) + jnp.log(1.0 + jnp.exp(-jnp.abs(drive)))
-            current = (saturation * (softplus - LOG_TWO)).astype(jnp.bfloat16)
-            charge = (junction * voltage * lax.rsqrt(1.0 + voltage * voltage)).astype(jnp.bfloat16)
-            samples = jnp.concatenate([current, charge], axis=0)
-            out_ref[point, :, span] += jnp.dot(
-                analysis_ref[...], samples, preferred_element_type=jnp.float32
+            out_ref[point, :, span] += evaluate(
+                spectra, synthesis_ref[...], analysis_ref[...], *scales
             )
         return carry
 
-    lax.fori_loop(0, chunks, nonlinear, 0)
+    lax.fori_loop(0, chunks - 1, nonlinear, 0)
+    first = blocks - unit
+    tail_ref[0] = pool_ref[first : first + unit]
+    for by in range(1, shares):
+        exchange(chunks - 1, by).wait_recv()
+        tail_ref[by] = arrived_ref[by - 1, first : first + unit]
 
     def drain(chunk, carry):
         for by in range(1, shares):
@@ -290,31 +341,37 @@
     chunks = blocks // unit
     slots, count = halo_list.shape[2], neighbour_slot.shape[1]
     directions = len(OFFSETS)
+    pieces = 2 if rows % 16 == 0 else 1
     height = points * rows
     x = jnp.transpose(spectrum, (1, 0, 2))
     injected = jnp.transpose(source, (1, 0, 2))
     synthesis, analysis = (jnp.asarray(t) for t in fourier_tables(length, shares))
     scales = [v.reshape(blocks, LANES) for v in (capacitance, saturation, steepness, junction)]
-    smem = pl.BlockSpec(memory_space=pltpu.SMEM)
+    vmem = pl.BlockSpec(memory_space=pltpu.VMEM)
     hbm = pl.BlockSpec(memory_space=pltpu.HBM)
     bf16, f32 = jnp.bfloat16, jnp.float32
-    total = pl.pallas_call(
+    held = pl.pallas_call(
         functools.partial(kernel, unit),
-        in_specs=[smem, smem] + [hbm] * 9,
-        out_specs=pl.BlockSpec(memory_space=pltpu.VMEM),
-        out_shape=pltpu.VMEM((points, rows, nodes), f32),
-        scratch_shapes=[
+        in_specs=[hbm] * 11,
+        out_specs=[vmem] * 5,
+        out_shape=[
             pltpu.VMEM((points, rows, nodes), f32),
-            pltpu.VMEM((blocks, count, LANES, LANES), bf16),
+            pltpu.VMEM((shares, unit, height, LANES), bf16),
             pltpu.VMEM((length, 2 * length), bf16),
             pltpu.VMEM((rows, 2 * length), bf16),
             pltpu.VMEM((4, blocks, LANES), f32),
+        ],
+        scratch_shapes=[
+            pltpu.SMEM((directions, slots, halo_list.shape[0]), jnp.int32),
+            pltpu.SMEM((count, blocks), jnp.int32),
+            pltpu.VMEM((points, rows, nodes), f32),
+            pltpu.VMEM((blocks, count, LANES, LANES), bf16),
             pltpu.VMEM((blocks + directions * slots + 1, height, LANES), bf16),
             pltpu.VMEM((shares - 1, blocks, height, LANES), bf16),
             pltpu.VMEM((directions, slots, height, LANES), bf16),
             pltpu.VMEM((directions, slots, height, LANES), bf16),
             pltpu.SemaphoreType.DMA((chunks,)),
-            pltpu.SemaphoreType.DMA((8,)),
+            pltpu.SemaphoreType.DMA((10,)),
             pltpu.SemaphoreType.DMA((shares - 1, chunks)),
             pltpu.SemaphoreType.DMA((shares - 1, chunks)),
             pltpu.SemaphoreType.DMA((directions,)),
@@ -330,15 +387,35 @@
         ),
         name="residual",
     )(
-        jnp.transpose(halo_list, (1, 2, 0)),
-        neighbour_slot.T,
-        x,
-        injected,
-        coupling,
-        synthesis,
-        analysis,
-        *scales,
+        *[
+            pltpu.with_memory_space_constraint(value, pltpu.HBM)
+            for value in (
+                jnp.transpose(halo_list, (1, 2, 0)),
+                neighbour_slot.T,
+                x,
+                injected,
+                coupling,
+                synthesis,
+                analysis,
+                *scales,
+            )
+        ]
     )
+    total = pl.pallas_call(
+        functools.partial(finish_kernel, pieces),
+        in_specs=[vmem] * 5,
+        out_specs=hbm,
+        out_shape=pltpu.HBM((points, rows, nodes), f32),
+        scratch_shapes=[
+            pltpu.VMEM((points, rows, unit * LANES), f32),
+            pltpu.SemaphoreType.DMA((points * pieces + 1,)),
+        ],
+        compiler_params=pltpu.CompilerParams(vmem_limit_bytes=8 << 20),
+        cost_estimate=pl.CostEstimate(
+            flops=6 * height * unit * LANES * length, bytes_accessed=x.size * 4, transcendentals=0
+        ),
+        name="finish",
+    )(*[pltpu.with_memory_space_constraint(value, pltpu.VMEM) for value in held])
     return jnp.transpose(total, (1, 0, 2))
 
 

time: 71.8 us -> 59.4 us (0.83)
  the two profiles are of different devices: /device:TPU:0 before, /device:TPU:1 now
where the time goes in v1:
time: 59.4 us; the launch traced here: 58.3 us
  Pallas kernels  58.3 us (98%)
    pallas_call x1, Pallas kernels, local_part(): pl.pallas_call(functools.partial(kernel, unit), in_specs=[hbm] * 11, out_...  56 us
    pallas_call x1, Pallas kernels, local_part(): pl.pallas_call(functools.partial(finish_kernel, pieces), in_specs=[vmem]...  2.24 us

profile of v1, /device:TPU:1, one launch (start us, length us, event | category | flops | bytes accessed | tf_op | source)
XLA Modules:
  0.0 58.3 jit_solution(11326711927311421613)
XLA Ops:
  0.0 56.0 %residual.1 = (f32[3,64,6144]{2,1,0:T(8,128)S(1)}, bf16[2,2,192,128]{3,2,1,0:T(8,128)(2,1)S(1)}, bf16[128,256]{1,0:T(8,128)(2,1)S(1)}, bf16[64,256]{1,0:T(8,128)(2,1)S(1)}, f32[4,48,128]{2,1,0:T(8,128)S(1)}) custom-call(s32[4,4,16]{2,1,0:T(4,128)} %bitcast.15, s32[4,48]{1,0:T(4,128)} %bitcast.16, f32[3,64,6144]{2,1,0:T(8,128)} %bitcast.9, ...), custom_call_target="tpu_custom_call" | custom-call | flops 2113929216 | bytes 20447232 | tf_op jit(solution)/shard_map/residual/pallas_call | solution.py:353
  56.0 2.2 %finish.1 = f32[3,64,6144]{2,1,0:T(8,128)} custom-call(f32[3,64,6144]{2,1,0:T(8,128)S(1)} %get-tuple-element.10.total_ref, bf16[2,2,192,128]{3,2,1,0:T(8,128)(2,1)S(1)} %get-tuple-element.11.tail_ref, bf16[128,256]{1,0:T(8,128)(2,1)S(1)} %get-tuple-element.12.synthesis_ref, bf16[64,256]{1,0:T(8,128)(2,1)S(1)} %get-tuple-element.13.analysis_ref, ...), custom_call_target="tpu_custom_call" | custom-call | flops 37748736 | bytes 4718592 | tf_op jit(solution)/shard_map/finish/pallas_call | solution.py:404

commit v2 on v1

--- a/solution.py
+++ b/solution.py
@@ -10,6 +10,7 @@
 
 LOG_TWO = 0.6931471805599453
 OFFSETS = (-2, -1, 1, 2)
+CUTS = (0, 2, 14, 26, 38, 44, 46, 48)
 LANES = 128
 VMEM_BYTES = 36 << 20
 MESH = pl.DeviceIdType.MESH
@@ -90,6 +91,7 @@
 
 def kernel(
     unit,
+    bounds,
     list_hbm,
     slot_hbm,
     x_hbm,
@@ -123,8 +125,7 @@
 ):
     points, rows, nodes = x_ref.shape
     blocks = nodes // LANES
-    width = unit * LANES
-    chunks = blocks // unit
+    chunks = len(bounds) - 1
     count, slots = coupling_ref.shape[1], list_ref.shape[1]
     shares, devices = lax.axis_size("harm"), lax.axis_size("node")
     me, place = lax.axis_index("harm"), lax.axis_index("node")
@@ -133,25 +134,24 @@
     def on_mesh(device):
         return jnp.logical_and(device >= 0, device < devices)
 
-    def columns(chunk):
-        return pl.ds(pl.multiple_of(chunk * width, width), width)
-
     def load(chunk):
-        span = columns(chunk)
+        span = slice(bounds[chunk] * LANES, bounds[chunk + 1] * LANES)
         return pltpu.make_async_copy(
             x_hbm.at[:, :, span], x_ref.at[:, :, span], x_sem.at[chunk]
         )
 
-    def exchange(chunk, by):
-        part = pl.ds(chunk * unit, unit)
+    def exchange(low, high, by, recv):
         return pltpu.make_async_remote_copy(
-            src_ref=pool_ref.at[part],
-            dst_ref=arrived_ref.at[by - 1, part],
-            send_sem=send_sem.at[by - 1, chunk],
-            recv_sem=recv_sem.at[by - 1, chunk],
+            src_ref=pool_ref.at[low:high],
+            dst_ref=arrived_ref.at[by - 1, low:high],
+            send_sem=send_sem.at[by - 1],
+            recv_sem=recv_sem.at[by - 1, recv],
             device_id={"harm": lax.rem(me + by, shares)},
             device_id_type=MESH,
         )
+
+    def part(chunk, by):
+        return exchange(bounds[chunk], bounds[chunk + 1], by, chunk)
 
     def halo(direction, device):
         return pltpu.make_async_remote_copy(
@@ -179,58 +179,55 @@
                 barrier, inc=1, device_id={"node": place + offset}, device_id_type=MESH
             )
 
-    def start_load(chunk, carry):
+    for chunk in range(chunks):
         load(chunk).start()
-        return carry
-
-    lax.fori_loop(0, chunks, start_load, 0)
-    local = [
+    tables = [
         pltpu.make_async_copy(source, target, local_sem.at[i])
+        for i, (source, target) in enumerate([(list_hbm, list_ref), (slot_hbm, slot_ref)])
+    ]
+    large = [
+        pltpu.make_async_copy(source, target, local_sem.at[i + 2])
         for i, (source, target) in enumerate(
             [
-                (list_hbm, list_ref),
-                (slot_hbm, slot_ref),
                 (source_hbm, out_ref),
                 (coupling_hbm, coupling_ref),
-                (capacitance_hbm, scale_ref.at[0]),
-                (saturation_hbm, scale_ref.at[1]),
-                (steepness_hbm, scale_ref.at[2]),
-                (junction_hbm, scale_ref.at[3]),
                 (synthesis_hbm.at[me], synthesis_ref),
                 (analysis_hbm.at[me], analysis_ref),
             ]
         )
     ]
-    local[0].start()
-    local[1].start()
+    scales = [
+        pltpu.make_async_copy(source, scale_ref.at[i], local_sem.at[6])
+        for i, source in enumerate([capacitance_hbm, saturation_hbm, steepness_hbm, junction_hbm])
+    ]
+    for copy in tables:
+        copy.start()
+
+    def round_block(block, carry):
+        span = pl.ds(pl.multiple_of(block * LANES, LANES), LANES)
+        for point in range(points):
+            pool_ref[block, point * rows : (point + 1) * rows, :] = x_ref[point, :, span].astype(
+                jnp.bfloat16
+            )
+        return carry
 
     def round_chunk(chunk):
         load(chunk).wait()
-        for inner in range(unit):
-            block = chunk * unit + inner
-            span = pl.ds(pl.multiple_of(block * LANES, LANES), LANES)
-            for point in range(points):
-                pool_ref[block, point * rows : (point + 1) * rows, :] = x_ref[
-                    point, :, span
-                ].astype(jnp.bfloat16)
+        lax.fori_loop(bounds[chunk], bounds[chunk + 1], round_block, 0, unroll=unit)
 
     def send(chunk):
         for by in range(1, shares):
-            exchange(chunk, by).start()
+            part(chunk, by).start()
 
     round_chunk(0)
-    for copy in local[2:]:
+    for copy in large + scales:
         copy.start()
     pl.semaphore_wait(barrier, greeted)
-
-    def advance(chunk, carry):
+    for chunk in range(1, chunks):
         round_chunk(chunk)
         send(chunk - 1)
-        return carry
-
-    lax.fori_loop(1, chunks, advance, 0)
-    local[0].wait()
-    local[1].wait()
+    for copy in tables:
+        copy.wait()
     for direction in range(len(OFFSETS)):
         for slot in range(slots):
             packed_ref[direction, slot] = pool_ref[list_ref[direction, slot, place]]
@@ -242,8 +239,9 @@
             halo(direction, place + offset).start()
 
     pool_ref[blocks + len(OFFSETS) * slots] = jnp.zeros(pool_ref.shape[1:], pool_ref.dtype)
-    for copy in local[2:]:
+    for copy in large:
         copy.wait()
+    pltpu.make_async_copy(scale_ref, scale_ref, local_sem.at[6]).wait()
     for direction, offset in enumerate(OFFSETS):
         first = blocks + direction * slots
         there = on_mesh(place - offset)
@@ -284,12 +282,10 @@
 
     lax.fori_loop(0, blocks, couple, 0, unroll=unit)
 
-    def nonlinear(chunk, carry):
-        for by in range(1, shares):
-            exchange(chunk, by).wait_recv()
-        ids = [chunk * unit + inner for inner in range(unit)]
-        scales = [widen(scale_ref, index, ids) for index in (1, 2, 3)]
-        span = columns(chunk)
+    def nonlinear(group, carry):
+        ids = [group * unit + inner for inner in range(unit)]
+        factors = [widen(scale_ref, index, ids) for index in (1, 2, 3)]
+        span = pl.ds(pl.multiple_of(group * unit * LANES, unit * LANES), unit * LANES)
         for point in range(points):
             held = slice(point * rows, (point + 1) * rows)
             spectra = [jnp.concatenate([pool_ref[block, held, :] for block in ids], axis=1)]
@@ -298,23 +294,22 @@
                     jnp.concatenate([arrived_ref[by - 1, block, held, :] for block in ids], axis=1)
                 )
             out_ref[point, :, span] += evaluate(
-                spectra, synthesis_ref[...], analysis_ref[...], *scales
+                spectra, synthesis_ref[...], analysis_ref[...], *factors
             )
         return carry
 
-    lax.fori_loop(0, chunks - 1, nonlinear, 0)
-    first = blocks - unit
-    tail_ref[0] = pool_ref[first : first + unit]
+    for chunk in range(chunks - 1):
+        for by in range(1, shares):
+            part(chunk, by).wait_recv()
+        lax.fori_loop(bounds[chunk] // unit, bounds[chunk + 1] // unit, nonlinear, 0)
+    first = bounds[chunks - 1]
+    tail_ref[0] = pool_ref[first:blocks]
     for by in range(1, shares):
-        exchange(chunks - 1, by).wait_recv()
-        tail_ref[by] = arrived_ref[by - 1, first : first + unit]
-
-    def drain(chunk, carry):
-        for by in range(1, shares):
-            exchange(chunk, by).wait_send()
-        return carry
-
-    lax.fori_loop(0, chunks, drain, 0)
+        part(chunks - 1, by).wait_recv()
+        tail_ref[by] = arrived_ref[by - 1, first:blocks]
+
+    for by in range(1, shares):
+        exchange(0, blocks, by, 0).wait_send()
     for direction, offset in enumerate(OFFSETS):
 
         @pl.when(on_mesh(place + offset))
@@ -338,10 +333,11 @@
     length = rows * shares
     blocks = nodes // LANES
     unit = 2 if blocks % 2 == 0 else 1
-    chunks = blocks // unit
+    bounds = sorted({cut * blocks // CUTS[-1] // unit * unit for cut in CUTS})
+    chunks, last = len(bounds) - 1, blocks - bounds[-2]
     slots, count = halo_list.shape[2], neighbour_slot.shape[1]
     directions = len(OFFSETS)
-    pieces = 2 if rows % 16 == 0 else 1
+    pieces = 1
     height = points * rows
     x = jnp.transpose(spectrum, (1, 0, 2))
     injected = jnp.transpose(source, (1, 0, 2))
@@ -351,12 +347,12 @@
     hbm = pl.BlockSpec(memory_space=pltpu.HBM)
     bf16, f32 = jnp.bfloat16, jnp.float32
     held = pl.pallas_call(
-        functools.partial(kernel, unit),
+        functools.partial(kernel, unit, bounds),
         in_specs=[hbm] * 11,
         out_specs=[vmem] * 5,
         out_shape=[
             pltpu.VMEM((points, rows, nodes), f32),
-            pltpu.VMEM((shares, unit, height, LANES), bf16),
+            pltpu.VMEM((shares, last, height, LANES), bf16),
             pltpu.VMEM((length, 2 * length), bf16),
             pltpu.VMEM((rows, 2 * length), bf16),
             pltpu.VMEM((4, blocks, LANES), f32),
@@ -371,8 +367,8 @@
             pltpu.VMEM((directions, slots, height, LANES), bf16),
             pltpu.VMEM((directions, slots, height, LANES), bf16),
             pltpu.SemaphoreType.DMA((chunks,)),
-            pltpu.SemaphoreType.DMA((10,)),
-            pltpu.SemaphoreType.DMA((shares - 1, chunks)),
+            pltpu.SemaphoreType.DMA((7,)),
+            pltpu.SemaphoreType.DMA((shares - 1,)),
             pltpu.SemaphoreType.DMA((shares - 1, chunks)),
             pltpu.SemaphoreType.DMA((directions,)),
             pltpu.SemaphoreType.DMA((directions,)),
@@ -407,12 +403,12 @@
         out_specs=hbm,
         out_shape=pltpu.HBM((points, rows, nodes), f32),
         scratch_shapes=[
-            pltpu.VMEM((points, rows, unit * LANES), f32),
+            pltpu.VMEM((points, rows, last * LANES), f32),
             pltpu.SemaphoreType.DMA((points * pieces + 1,)),
         ],
         compiler_params=pltpu.CompilerParams(vmem_limit_bytes=8 << 20),
         cost_estimate=pl.CostEstimate(
-            flops=6 * height * unit * LANES * length, bytes_accessed=x.size * 4, transcendentals=0
+            flops=6 * height * last * LANES * length, bytes_accessed=x.size * 4, transcendentals=0
         ),
         name="finish",
     )(*[pltpu.with_memory_space_constraint(value, pltpu.VMEM) for value in held])

time: 59.4 us -> 58.8 us (0.990)
  Pallas kernels: 58.3 us -> 57.7 us
where the time goes in v2:
time: 58.8 us; the launch traced here: 57.7 us
  Pallas kernels  57.7 us (98%)
    pallas_call x1, Pallas kernels, local_part(): pl.pallas_call(functools.partial(kernel, unit, bounds), in_specs=[hbm] *...  55.5 us
    pallas_call x1, Pallas kernels, local_part(): pl.pallas_call(functools.partial(finish_kernel, pieces), in_specs=[vmem]...  2.21 us

profile of v2, /device:TPU:1, one launch (start us, length us, event | category | flops | bytes accessed | tf_op | source)
XLA Modules:
  0.0 57.7 jit_solution(13007415064050523100)
XLA Ops:
  0.0 55.5 %residual.1 = (f32[3,64,6144]{2,1,0:T(8,128)S(1)}, bf16[2,2,192,128]{3,2,1,0:T(8,128)(2,1)S(1)}, bf16[128,256]{1,0:T(8,128)(2,1)S(1)}, bf16[64,256]{1,0:T(8,128)(2,1)S(1)}, f32[4,48,128]{2,1,0:T(8,128)S(1)}) custom-call(s32[4,4,16]{2,1,0:T(4,128)} %bitcast.15, s32[4,48]{1,0:T(4,128)} %bitcast.16, f32[3,64,6144]{2,1,0:T(8,128)} %bitcast.9, ...), custom_call_target="tpu_custom_call" | custom-call | flops 2113929216 | bytes 20447232 | tf_op jit(solution)/shard_map/residual/pallas_call | solution.py:349
  55.5 2.2 %finish.1 = f32[3,64,6144]{2,1,0:T(8,128)} custom-call(f32[3,64,6144]{2,1,0:T(8,128)S(1)} %get-tuple-element.10.total_ref, bf16[2,2,192,128]{3,2,1,0:T(8,128)(2,1)S(1)} %get-tuple-element.11.tail_ref, bf16[128,256]{1,0:T(8,128)(2,1)S(1)} %get-tuple-element.12.synthesis_ref, bf16[64,256]{1,0:T(8,128)(2,1)S(1)} %get-tuple-element.13.analysis_ref, ...), custom_call_target="tpu_custom_call" | custom-call | flops 37748736 | bytes 4718592 | tf_op jit(solution)/shard_map/finish/pallas_call | solution.py:400

commit v3 on v2

--- a/solution.py
+++ b/solution.py
@@ -122,6 +122,10 @@
     recv_sem,
     halo_send_sem,
     halo_recv_sem,
+    ready_sem,
+    start_sem,
+    group_sem,
+    halo_sem,
 ):
     points, rows, nodes = x_ref.shape
     blocks = nodes // LANES
@@ -163,23 +167,30 @@
             device_id_type=MESH,
         )
 
+    root = me == 0
+    member = jnp.logical_not(root)
+    group = [{"harm": other} for other in range(1, shares)]
     barrier = pltpu.get_barrier_semaphore()
-    for by in range(1, shares):
-        pl.semaphore_signal(
-            barrier, inc=1, device_id={"harm": lax.rem(me + by, shares)}, device_id_type=MESH
-        )
-    greeted = shares - 1
-    for offset in OFFSETS:
-        there = on_mesh(place + offset)
-        greeted = greeted + there.astype(jnp.int32)
-
-        @pl.when(there)
-        def _():
-            pl.semaphore_signal(
-                barrier, inc=1, device_id={"node": place + offset}, device_id_type=MESH
-            )
-
-    for chunk in range(chunks):
+    load(0).start()
+
+    def signal(semaphore, device):
+        pl.semaphore_signal(semaphore, inc=1, device_id=device, device_id_type=MESH)
+
+    @pl.when(root)
+    def _():
+        for other in group:
+            signal(barrier, other)
+
+    def greet(semaphore):
+        for offset in OFFSETS:
+
+            @pl.when(jnp.logical_and(root, on_mesh(place + offset)))
+            def _():
+                signal(semaphore, {"node": place + offset})
+
+    greet(barrier)
+    greeted = sum(on_mesh(place + offset).astype(jnp.int32) for offset in OFFSETS)
+    for chunk in range(1, chunks):
         load(chunk).start()
     tables = [
         pltpu.make_async_copy(source, target, local_sem.at[i])
@@ -219,10 +230,29 @@
         for by in range(1, shares):
             part(chunk, by).start()
 
+    @pl.when(member)
+    def _():
+        pl.semaphore_wait(barrier, 1)
+        signal(ready_sem, {"harm": 0})
+
     round_chunk(0)
     for copy in large + scales:
         copy.start()
-    pl.semaphore_wait(barrier, greeted)
+
+    @pl.when(root)
+    def _():
+        pl.semaphore_wait(barrier, greeted)
+        pl.semaphore_wait(ready_sem, shares - 1)
+        if shares > 2:
+            for other in group:
+                signal(start_sem, other)
+
+    if shares > 2:
+
+        @pl.when(member)
+        def _():
+            pl.semaphore_wait(start_sem, 1)
+
     for chunk in range(1, chunks):
         round_chunk(chunk)
         send(chunk - 1)
@@ -232,6 +262,18 @@
         for slot in range(slots):
             packed_ref[direction, slot] = pool_ref[list_ref[direction, slot, place]]
     send(chunks - 1)
+    greet(group_sem)
+
+    @pl.when(root)
+    def _():
+        pl.semaphore_wait(group_sem, greeted)
+        for other in group:
+            signal(halo_sem, other)
+
+    @pl.when(member)
+    def _():
+        pl.semaphore_wait(halo_sem, 1)
+
     for direction, offset in enumerate(OFFSETS):
 
         @pl.when(on_mesh(place + offset))
@@ -372,7 +414,8 @@
             pltpu.SemaphoreType.DMA((shares - 1, chunks)),
             pltpu.SemaphoreType.DMA((directions,)),
             pltpu.SemaphoreType.DMA((directions,)),
-        ],
+        ]
+        + [pltpu.SemaphoreType.REGULAR] * 4,
         compiler_params=pltpu.CompilerParams(
             collective_id=0, has_side_effects=True, vmem_limit_bytes=VMEM_BYTES
         ),

time: 58.8 us -> 58.4 us (level)
  the two profiles are of different devices: /device:TPU:1 before, /device:TPU:0 now
where the time goes in v3:
time: 58.4 us; the launch traced here: 58.3 us
  Pallas kernels  58.3 us (100%)
    pallas_call x1, Pallas kernels, local_part(): pl.pallas_call(functools.partial(kernel, unit, bounds), in_specs=[hbm] *...  56.1 us
    pallas_call x1, Pallas kernels, local_part(): pl.pallas_call(functools.partial(finish_kernel, pieces), in_specs=[vmem]...  2.21 us

profile of v3, /device:TPU:0, one launch (start us, length us, event | category | flops | bytes accessed | tf_op | source)
XLA Modules:
  0.0 58.3 jit_solution(15602425277589641659)
XLA Ops:
  0.0 56.1 %residual.1 = (f32[3,64,6144]{2,1,0:T(8,128)S(1)}, bf16[2,2,192,128]{3,2,1,0:T(8,128)(2,1)S(1)}, bf16[128,256]{1,0:T(8,128)(2,1)S(1)}, bf16[64,256]{1,0:T(8,128)(2,1)S(1)}, f32[4,48,128]{2,1,0:T(8,128)S(1)}) custom-call(s32[4,4,16]{2,1,0:T(4,128)} %bitcast.15, s32[4,48]{1,0:T(4,128)} %bitcast.16, f32[3,64,6144]{2,1,0:T(8,128)} %bitcast.9, ...), custom_call_target="tpu_custom_call" | custom-call | flops 2113929216 | bytes 20447232 | tf_op jit(solution)/shard_map/residual/pallas_call | solution.py:391
  56.1 2.2 %finish.1 = f32[3,64,6144]{2,1,0:T(8,128)} custom-call(f32[3,64,6144]{2,1,0:T(8,128)S(1)} %get-tuple-element.10.total_ref, bf16[2,2,192,128]{3,2,1,0:T(8,128)(2,1)S(1)} %get-tuple-element.11.tail_ref, bf16[128,256]{1,0:T(8,128)(2,1)S(1)} %get-tuple-element.12.synthesis_ref, bf16[64,256]{1,0:T(8,128)(2,1)S(1)} %get-tuple-element.13.analysis_ref, ...), custom_call_target="tpu_custom_call" | custom-call | flops 37748736 | bytes 4718592 | tf_op jit(solution)/shard_map/finish/pallas_call | solution.py:443

commit v4 on v3

--- a/solution.py
+++ b/solution.py
@@ -10,7 +10,7 @@
 
 LOG_TWO = 0.6931471805599453
 OFFSETS = (-2, -1, 1, 2)
-CUTS = (0, 2, 14, 26, 38, 44, 46, 48)
+CUTS = (0, 2, 4, 14, 26, 38, 44, 46, 48)
 LANES = 128
 VMEM_BYTES = 36 << 20
 MESH = pl.DeviceIdType.MESH
@@ -56,22 +56,15 @@
     return jnp.concatenate(parts, axis=1)
 
 
-def finish_kernel(pieces, total_ref, tail_ref, synthesis_ref, analysis_ref, scale_ref, out_hbm, last_ref, sem):
+def finish_kernel(total_ref, tail_ref, synthesis_ref, analysis_ref, scale_ref, out_hbm, last_ref, sem):
     points, rows, nodes = total_ref.shape
     shares, unit = tail_ref.shape[:2]
     blocks = nodes // LANES
     done = nodes - unit * LANES
-    copies = []
-    for point in range(points):
-        for piece in range(pieces):
-            part = (point, slice(piece * rows // pieces, (piece + 1) * rows // pieces), slice(0, done))
-            copies.append(
-                pltpu.make_async_copy(
-                    total_ref.at[part], out_hbm.at[part], sem.at[point * pieces + piece]
-                )
-            )
-    for copy in copies:
-        copy.start()
+    bulk = pltpu.make_async_copy(
+        total_ref.at[:, :, :done], out_hbm.at[:, :, :done], sem.at[0]
+    )
+    bulk.start()
     ids = range(blocks - unit, blocks)
     scales = [widen(scale_ref, index, ids) for index in (1, 2, 3)]
     for point in range(points):
@@ -83,10 +76,10 @@
         last_ref[point] = total_ref[point, :, done:] + evaluate(
             spectra, synthesis_ref[...], analysis_ref[...], *scales
         )
-    copy = pltpu.make_async_copy(last_ref, out_hbm.at[:, :, done:], sem.at[points * pieces])
+    copy = pltpu.make_async_copy(last_ref, out_hbm.at[:, :, done:], sem.at[1])
     copy.start()
-    for each in copies + [copy]:
-        each.wait()
+    bulk.wait()
+    copy.wait()
 
 
 def kernel(
@@ -130,6 +123,8 @@
     points, rows, nodes = x_ref.shape
     blocks = nodes // LANES
     chunks = len(bounds) - 1
+    loads = bounds[:3] + bounds[-1:]
+    groups = bounds[:1] + bounds[3:]
     count, slots = coupling_ref.shape[1], list_ref.shape[1]
     shares, devices = lax.axis_size("harm"), lax.axis_size("node")
     me, place = lax.axis_index("harm"), lax.axis_index("node")
@@ -138,10 +133,10 @@
     def on_mesh(device):
         return jnp.logical_and(device >= 0, device < devices)
 
-    def load(chunk):
-        span = slice(bounds[chunk] * LANES, bounds[chunk + 1] * LANES)
+    def load(step):
+        span = slice(loads[step] * LANES, loads[step + 1] * LANES)
         return pltpu.make_async_copy(
-            x_hbm.at[:, :, span], x_ref.at[:, :, span], x_sem.at[chunk]
+            x_hbm.at[:, :, span], x_ref.at[:, :, span], x_sem.at[step]
         )
 
     def exchange(low, high, by, recv):
@@ -154,8 +149,11 @@
             device_id_type=MESH,
         )
 
-    def part(chunk, by):
-        return exchange(bounds[chunk], bounds[chunk + 1], by, chunk)
+    def group_of(block):
+        return sum(block >= end for end in groups[1:])
+
+    def arrival(group, by):
+        return exchange(groups[group], groups[group + 1], by, group)
 
     def halo(direction, device):
         return pltpu.make_async_remote_copy(
@@ -169,7 +167,7 @@
 
     root = me == 0
     member = jnp.logical_not(root)
-    group = [{"harm": other} for other in range(1, shares)]
+    members = [{"harm": other} for other in range(1, shares)]
     barrier = pltpu.get_barrier_semaphore()
     load(0).start()
 
@@ -178,7 +176,7 @@
 
     @pl.when(root)
     def _():
-        for other in group:
+        for other in members:
             signal(barrier, other)
 
     def greet(semaphore):
@@ -190,8 +188,8 @@
 
     greet(barrier)
     greeted = sum(on_mesh(place + offset).astype(jnp.int32) for offset in OFFSETS)
-    for chunk in range(1, chunks):
-        load(chunk).start()
+    for step in range(1, len(loads) - 1):
+        load(step).start()
     tables = [
         pltpu.make_async_copy(source, target, local_sem.at[i])
         for i, (source, target) in enumerate([(list_hbm, list_ref), (slot_hbm, slot_ref)])
@@ -223,12 +221,13 @@
         return carry
 
     def round_chunk(chunk):
-        load(chunk).wait()
+        if chunk < len(loads) - 1:
+            load(chunk).wait()
         lax.fori_loop(bounds[chunk], bounds[chunk + 1], round_block, 0, unroll=unit)
 
-    def send(chunk):
+    def send(low, high):
         for by in range(1, shares):
-            part(chunk, by).start()
+            exchange(low, high, by, group_of(low)).start()
 
     @pl.when(member)
     def _():
@@ -244,7 +243,7 @@
         pl.semaphore_wait(barrier, greeted)
         pl.semaphore_wait(ready_sem, shares - 1)
         if shares > 2:
-            for other in group:
+            for other in members:
                 signal(start_sem, other)
 
     if shares > 2:
@@ -255,19 +254,31 @@
 
     for chunk in range(1, chunks):
         round_chunk(chunk)
-        send(chunk - 1)
+        send(bounds[chunk - 1], bounds[chunk])
     for copy in tables:
         copy.wait()
     for direction in range(len(OFFSETS)):
         for slot in range(slots):
             packed_ref[direction, slot] = pool_ref[list_ref[direction, slot, place]]
-    send(chunks - 1)
+    late = lax.rem(place, 2) == 1
+    final, kept = bounds[-2], blocks - 1
+
+    @pl.when(jnp.logical_not(late))
+    def _():
+        send(final, blocks)
+
+    if final < kept:
+
+        @pl.when(late)
+        def _():
+            send(final, kept)
+
     greet(group_sem)
 
     @pl.when(root)
     def _():
         pl.semaphore_wait(group_sem, greeted)
-        for other in group:
+        for other in members:
             signal(halo_sem, other)
 
     @pl.when(member)
@@ -340,15 +351,20 @@
             )
         return carry
 
-    for chunk in range(chunks - 1):
+    for group in range(len(groups) - 2):
         for by in range(1, shares):
-            part(chunk, by).wait_recv()
-        lax.fori_loop(bounds[chunk] // unit, bounds[chunk + 1] // unit, nonlinear, 0)
-    first = bounds[chunks - 1]
-    tail_ref[0] = pool_ref[first:blocks]
+            arrival(group, by).wait_recv()
+        if group == len(groups) - 3:
+
+            @pl.when(late)
+            def _():
+                send(kept, blocks)
+
+        lax.fori_loop(groups[group] // unit, groups[group + 1] // unit, nonlinear, 0)
+    tail_ref[0] = pool_ref[final:blocks]
     for by in range(1, shares):
-        part(chunks - 1, by).wait_recv()
-        tail_ref[by] = arrived_ref[by - 1, first:blocks]
+        arrival(len(groups) - 2, by).wait_recv()
+        tail_ref[by] = arrived_ref[by - 1, final:blocks]
 
     for by in range(1, shares):
         exchange(0, blocks, by, 0).wait_send()
@@ -376,10 +392,9 @@
     blocks = nodes // LANES
     unit = 2 if blocks % 2 == 0 else 1
     bounds = sorted({cut * blocks // CUTS[-1] // unit * unit for cut in CUTS})
-    chunks, last = len(bounds) - 1, blocks - bounds[-2]
+    last = blocks - bounds[-2]
     slots, count = halo_list.shape[2], neighbour_slot.shape[1]
     directions = len(OFFSETS)
-    pieces = 1
     height = points * rows
     x = jnp.transpose(spectrum, (1, 0, 2))
     injected = jnp.transpose(source, (1, 0, 2))
@@ -408,10 +423,10 @@
             pltpu.VMEM((shares - 1, blocks, height, LANES), bf16),
             pltpu.VMEM((directions, slots, height, LANES), bf16),
             pltpu.VMEM((directions, slots, height, LANES), bf16),
-            pltpu.SemaphoreType.DMA((chunks,)),
+            pltpu.SemaphoreType.DMA((3,)),
             pltpu.SemaphoreType.DMA((7,)),
             pltpu.SemaphoreType.DMA((shares - 1,)),
-            pltpu.SemaphoreType.DMA((shares - 1, chunks)),
+            pltpu.SemaphoreType.DMA((shares - 1, len(bounds) - 3)),
             pltpu.SemaphoreType.DMA((directions,)),
             pltpu.SemaphoreType.DMA((directions,)),
         ]
@@ -441,13 +456,13 @@
         ]
     )
     total = pl.pallas_call(
-        functools.partial(finish_kernel, pieces),
+        finish_kernel,
         in_specs=[vmem] * 5,
         out_specs=hbm,
         out_shape=pltpu.HBM((points, rows, nodes), f32),
         scratch_shapes=[
             pltpu.VMEM((points, rows, last * LANES), f32),
-            pltpu.SemaphoreType.DMA((points * pieces + 1,)),
+            pltpu.SemaphoreType.DMA((2,)),
         ],
         compiler_params=pltpu.CompilerParams(vmem_limit_bytes=8 << 20),
         cost_estimate=pl.CostEstimate(

time: 58.4 us -> 57.3 us (0.981)
  the two profiles are of different devices: /device:TPU:0 before, /device:TPU:1 now
where the time goes in v4:
time: 57.3 us; the launch traced here: 57.2 us
  Pallas kernels  57.2 us (100%)
    pallas_call x1, Pallas kernels, local_part(): pl.pallas_call(functools.partial(kernel, unit, bounds), in_specs=[hbm] *...  55 us
    pallas_call x1, Pallas kernels, local_part(): pl.pallas_call(finish_kernel, in_specs=[vmem] * 5, out_specs=hbm, out_sha...  2.2 us

profile of v4, /device:TPU:1, one launch (start us, length us, event | category | flops | bytes accessed | tf_op | source)
XLA Modules:
  0.0 57.2 jit_solution(3117638505998931199)
XLA Ops:
  0.0 55.0 %residual.1 = (f32[3,64,6144]{2,1,0:T(8,128)S(1)}, bf16[2,2,192,128]{3,2,1,0:T(8,128)(2,1)S(1)}, bf16[128,256]{1,0:T(8,128)(2,1)S(1)}, bf16[64,256]{1,0:T(8,128)(2,1)S(1)}, f32[4,48,128]{2,1,0:T(8,128)S(1)}) custom-call(s32[4,4,16]{2,1,0:T(4,128)} %bitcast.15, s32[4,48]{1,0:T(4,128)} %bitcast.16, f32[3,64,6144]{2,1,0:T(8,128)} %bitcast.9, ...), custom_call_target="tpu_custom_call" | custom-call | flops 2113929216 | bytes 20447232 | tf_op jit(solution)/shard_map/residual/pallas_call | solution.py:406
  55.0 2.2 %finish.1 = f32[3,64,6144]{2,1,0:T(8,128)} custom-call(f32[3,64,6144]{2,1,0:T(8,128)S(1)} %get-tuple-element.10.total_ref, bf16[2,2,192,128]{3,2,1,0:T(8,128)(2,1)S(1)} %get-tuple-element.11.tail_ref, bf16[128,256]{1,0:T(8,128)(2,1)S(1)} %get-tuple-element.12.synthesis_ref, bf16[64,256]{1,0:T(8,128)(2,1)S(1)} %get-tuple-element.13.analysis_ref, ...), custom_call_target="tpu_custom_call" | custom-call | flops 37748736 | bytes 4718592 | tf_op jit(solution)/shard_map/finish/pallas_call | solution.py:458

commit v5 on v4

--- a/solution.py
+++ b/solution.py
@@ -10,7 +10,9 @@
 
 LOG_TWO = 0.6931471805599453
 OFFSETS = (-2, -1, 1, 2)
-CUTS = (0, 2, 4, 14, 26, 38, 44, 46, 48)
+CUTS = (0, 2, 4, 14, 26, 36)
+LATER = (36, 42, 46, 48)
+TOTAL = 48
 LANES = 128
 VMEM_BYTES = 36 << 20
 MESH = pl.DeviceIdType.MESH
@@ -56,13 +58,25 @@
     return jnp.concatenate(parts, axis=1)
 
 
-def finish_kernel(total_ref, tail_ref, synthesis_ref, analysis_ref, scale_ref, out_hbm, last_ref, sem):
-    points, rows, nodes = total_ref.shape
+def early_kernel(width, total_ref, out_hbm, token_ref, sem):
+    copy = pltpu.make_async_copy(
+        total_ref.at[:, :, :width], out_hbm.at[:, :, :width], sem.at[0]
+    )
+    copy.start()
+    token_ref[...] = jnp.zeros_like(token_ref)
+    copy.wait()
+
+
+def finish_kernel(
+    _, rest_ref, tail_ref, synthesis_ref, analysis_ref, scale_ref, out_hbm, last_ref, sem
+):
+    points, rows, width = rest_ref.shape
     shares, unit = tail_ref.shape[:2]
+    nodes = out_hbm.shape[2]
     blocks = nodes // LANES
-    done = nodes - unit * LANES
+    done, before = width - unit * LANES, nodes - width
     bulk = pltpu.make_async_copy(
-        total_ref.at[:, :, :done], out_hbm.at[:, :, :done], sem.at[0]
+        rest_ref.at[:, :, :done], out_hbm.at[:, :, before : before + done], sem.at[0]
     )
     bulk.start()
     ids = range(blocks - unit, blocks)
@@ -73,13 +87,96 @@
             jnp.concatenate([tail_ref[share, inner, held, :] for inner in range(unit)], axis=1)
             for share in range(shares)
         ]
-        last_ref[point] = total_ref[point, :, done:] + evaluate(
+        last_ref[point] = rest_ref[point, :, done:] + evaluate(
             spectra, synthesis_ref[...], analysis_ref[...], *scales
         )
-    copy = pltpu.make_async_copy(last_ref, out_hbm.at[:, :, done:], sem.at[1])
+    copy = pltpu.make_async_copy(last_ref, out_hbm.at[:, :, before + done :], sem.at[1])
     copy.start()
     bulk.wait()
     copy.wait()
+
+
+def later_kernel(
+    unit,
+    written,
+    bounds,
+    _,
+    total_ref,
+    pool_ref,
+    before_ref,
+    synthesis_ref,
+    analysis_ref,
+    scale_ref,
+    rest_ref,
+    tail_ref,
+    arrived_ref,
+    send_sem,
+    recv_sem,
+):
+    points, rows, nodes = total_ref.shape
+    blocks = nodes // LANES
+    shares = lax.axis_size("harm")
+    me = lax.axis_index("harm")
+    base = bounds[0]
+    barrier = pltpu.get_barrier_semaphore()
+    for by in range(1, shares):
+        pl.semaphore_signal(
+            barrier, inc=1, device_id={"harm": lax.rem(me + by, shares)}, device_id_type=MESH
+        )
+    pl.semaphore_wait(barrier, shares - 1)
+
+    def exchange(low, high, by, recv):
+        return pltpu.make_async_remote_copy(
+            src_ref=pool_ref.at[low:high],
+            dst_ref=arrived_ref.at[by - 1, low - base : high - base],
+            send_sem=send_sem.at[by - 1],
+            recv_sem=recv_sem.at[by - 1, recv],
+            device_id={"harm": lax.rem(me + by, shares)},
+            device_id_type=MESH,
+        )
+
+    pieces = list(zip(bounds[:-1], bounds[1:]))
+    for index, (low, high) in enumerate(pieces):
+        for by in range(1, shares):
+            exchange(low, high, by, index).start()
+
+    def nonlinear(source_ref, shift, group, carry):
+        ids = [group * unit + inner for inner in range(unit)]
+        factors = [widen(scale_ref, index, ids) for index in (1, 2, 3)]
+        width = unit * LANES
+        span = pl.ds(pl.multiple_of(group * width, width), width)
+        target = pl.ds(pl.multiple_of(group * width - written * LANES, width), width)
+        for point in range(points):
+            held = slice(point * rows, (point + 1) * rows)
+            spectra = [jnp.concatenate([pool_ref[block, held, :] for block in ids], axis=1)]
+            for by in range(1, shares):
+                spectra.append(
+                    jnp.concatenate(
+                        [source_ref[by - 1, block - shift, held, :] for block in ids], axis=1
+                    )
+                )
+            rest_ref[point, :, target] = total_ref[point, :, span] + evaluate(
+                spectra, synthesis_ref[...], analysis_ref[...], *factors
+            )
+        return carry
+
+    lax.fori_loop(
+        written // unit, base // unit, functools.partial(nonlinear, before_ref, 0), 0
+    )
+    final = bounds[-2]
+    rest_ref[:, :, (final - written) * LANES :] = total_ref[:, :, final * LANES :]
+    tail_ref[0] = pool_ref[final:blocks]
+    for index, (low, high) in enumerate(pieces):
+        for by in range(1, shares):
+            exchange(low, high, by, index).wait_recv()
+        if high < blocks:
+            lax.fori_loop(
+                low // unit, high // unit, functools.partial(nonlinear, arrived_ref, base), 0
+            )
+    for by in range(1, shares):
+        tail_ref[by] = arrived_ref[by - 1, final - base :]
+    for by in range(1, shares):
+        exchange(base, blocks, by, 0).wait_send()
 
 
 def kernel(
@@ -97,7 +194,8 @@
     steepness_hbm,
     junction_hbm,
     out_ref,
-    tail_ref,
+    pool_ref,
+    arrived_ref,
     synthesis_ref,
     analysis_ref,
     scale_ref,
@@ -105,8 +203,6 @@
     slot_ref,
     x_ref,
     coupling_ref,
-    pool_ref,
-    arrived_ref,
     packed_ref,
     halo_ref,
     x_sem,
@@ -123,7 +219,7 @@
     points, rows, nodes = x_ref.shape
     blocks = nodes // LANES
     chunks = len(bounds) - 1
-    loads = bounds[:3] + bounds[-1:]
+    loads = bounds[:3] + [blocks]
     groups = bounds[:1] + bounds[3:]
     count, slots = coupling_ref.shape[1], list_ref.shape[1]
     shares, devices = lax.axis_size("harm"), lax.axis_size("node")
@@ -234,12 +330,16 @@
         pl.semaphore_wait(barrier, 1)
         signal(ready_sem, {"harm": 0})
 
+    def start_large():
+        for copy in large + scales:
+            copy.start()
+
     round_chunk(0)
-    for copy in large + scales:
-        copy.start()
+    round_chunk(1)
 
     @pl.when(root)
     def _():
+        start_large()
         pl.semaphore_wait(barrier, greeted)
         pl.semaphore_wait(ready_sem, shares - 1)
         if shares > 2:
@@ -252,26 +352,25 @@
         def _():
             pl.semaphore_wait(start_sem, 1)
 
-    for chunk in range(1, chunks):
+    send(bounds[0], bounds[1])
+    pl.when(member)(start_large)
+    send(bounds[1], bounds[2])
+    for chunk in range(2, chunks):
         round_chunk(chunk)
-        send(bounds[chunk - 1], bounds[chunk])
+        if chunk > 2:
+            send(bounds[chunk - 1], bounds[chunk])
+    lax.fori_loop(bounds[-1], blocks, round_block, 0, unroll=unit)
     for copy in tables:
         copy.wait()
     for direction in range(len(OFFSETS)):
         for slot in range(slots):
             packed_ref[direction, slot] = pool_ref[list_ref[direction, slot, place]]
     late = lax.rem(place, 2) == 1
-    final, kept = bounds[-2], blocks - 1
+    kept = bounds[-2]
 
     @pl.when(jnp.logical_not(late))
     def _():
-        send(final, blocks)
-
-    if final < kept:
-
-        @pl.when(late)
-        def _():
-            send(final, kept)
+        send(kept, bounds[-1])
 
     greet(group_sem)
 
@@ -351,23 +450,20 @@
             )
         return carry
 
-    for group in range(len(groups) - 2):
+    last = len(groups) - 2
+    for group in range(last):
         for by in range(1, shares):
             arrival(group, by).wait_recv()
-        if group == len(groups) - 3:
-
-            @pl.when(late)
-            def _():
-                send(kept, blocks)
-
         lax.fori_loop(groups[group] // unit, groups[group + 1] // unit, nonlinear, 0)
-    tail_ref[0] = pool_ref[final:blocks]
+
+    @pl.when(late)
+    def _():
+        send(kept, bounds[-1])
+
     for by in range(1, shares):
-        arrival(len(groups) - 2, by).wait_recv()
-        tail_ref[by] = arrived_ref[by - 1, final:blocks]
-
+        arrival(last, by).wait_recv()
     for by in range(1, shares):
-        exchange(0, blocks, by, 0).wait_send()
+        exchange(0, bounds[-1], by, 0).wait_send()
     for direction, offset in enumerate(OFFSETS):
 
         @pl.when(on_mesh(place + offset))
@@ -391,8 +487,11 @@
     length = rows * shares
     blocks = nodes // LANES
     unit = 2 if blocks % 2 == 0 else 1
-    bounds = sorted({cut * blocks // CUTS[-1] // unit * unit for cut in CUTS})
-    last = blocks - bounds[-2]
+    bounds, later = (
+        sorted({cut * blocks // TOTAL // unit * unit for cut in cuts}) for cuts in (CUTS, LATER)
+    )
+    later[-1] = blocks
+    last, written = blocks - later[-2], bounds[-2]
     slots, count = halo_list.shape[2], neighbour_slot.shape[1]
     directions = len(OFFSETS)
     height = points * rows
@@ -406,10 +505,11 @@
     held = pl.pallas_call(
         functools.partial(kernel, unit, bounds),
         in_specs=[hbm] * 11,
-        out_specs=[vmem] * 5,
+        out_specs=[vmem] * 6,
         out_shape=[
             pltpu.VMEM((points, rows, nodes), f32),
-            pltpu.VMEM((shares, last, height, LANES), bf16),
+            pltpu.VMEM((blocks + directions * slots + 1, height, LANES), bf16),
+            pltpu.VMEM((shares - 1, blocks, height, LANES), bf16),
             pltpu.VMEM((length, 2 * length), bf16),
             pltpu.VMEM((rows, 2 * length), bf16),
             pltpu.VMEM((4, blocks, LANES), f32),
@@ -419,8 +519,6 @@
             pltpu.SMEM((count, blocks), jnp.int32),
             pltpu.VMEM((points, rows, nodes), f32),
             pltpu.VMEM((blocks, count, LANES, LANES), bf16),
-            pltpu.VMEM((blocks + directions * slots + 1, height, LANES), bf16),
-            pltpu.VMEM((shares - 1, blocks, height, LANES), bf16),
             pltpu.VMEM((directions, slots, height, LANES), bf16),
             pltpu.VMEM((directions, slots, height, LANES), bf16),
             pltpu.SemaphoreType.DMA((3,)),
@@ -455,21 +553,65 @@
             )
         ]
     )
+    total, pool, arrived, *tables = (
+        pltpu.with_memory_space_constraint(value, pltpu.VMEM) for value in held
+    )
+    early, token = pl.pallas_call(
+        functools.partial(early_kernel, written * LANES),
+        in_specs=[vmem],
+        out_specs=[hbm, vmem],
+        out_shape=[pltpu.HBM((points, rows, nodes), f32), pltpu.VMEM((8, LANES), f32)],
+        scratch_shapes=[pltpu.SemaphoreType.DMA((1,))],
+        compiler_params=pltpu.CompilerParams(vmem_limit_bytes=1 << 20),
+        cost_estimate=pl.CostEstimate(
+            flops=0, bytes_accessed=height * written * LANES * 4, transcendentals=0
+        ),
+        name="early",
+    )(total)
+    width = nodes - written * LANES
+    rest, tail = pl.pallas_call(
+        functools.partial(later_kernel, unit, written, later),
+        in_specs=[vmem] * 7,
+        out_specs=[vmem] * 2,
+        out_shape=[
+            pltpu.VMEM((points, rows, width), f32),
+            pltpu.VMEM((shares, last, height, LANES), bf16),
+        ],
+        scratch_shapes=[
+            pltpu.VMEM((shares - 1, blocks - later[0], height, LANES), bf16),
+            pltpu.SemaphoreType.DMA((shares - 1,)),
+            pltpu.SemaphoreType.DMA((shares - 1, len(later) - 1)),
+        ],
+        compiler_params=pltpu.CompilerParams(
+            collective_id=1, has_side_effects=True, vmem_limit_bytes=12 << 20
+        ),
+        cost_estimate=pl.CostEstimate(
+            flops=6 * height * width * length, bytes_accessed=0, transcendentals=0
+        ),
+        name="later",
+    )(pltpu.with_memory_space_constraint(token, pltpu.VMEM), total, pool, arrived, *tables)
     total = pl.pallas_call(
         finish_kernel,
-        in_specs=[vmem] * 5,
+        in_specs=[hbm] + [vmem] * 5,
         out_specs=hbm,
         out_shape=pltpu.HBM((points, rows, nodes), f32),
         scratch_shapes=[
             pltpu.VMEM((points, rows, last * LANES), f32),
             pltpu.SemaphoreType.DMA((2,)),
         ],
+        input_output_aliases={0: 0},
         compiler_params=pltpu.CompilerParams(vmem_limit_bytes=8 << 20),
         cost_estimate=pl.CostEstimate(
-            flops=6 * height * last * LANES * length, bytes_accessed=x.size * 4, transcendentals=0
+            flops=6 * height * last * LANES * length,
+            bytes_accessed=height * width * 4,
+            transcendentals=0,
         ),
         name="finish",
-    )(*[pltpu.with_memory_space_constraint(value, pltpu.VMEM) for value in held])
+    )(
+        early,
+        *[pltpu.with_memory_space_constraint(value, pltpu.VMEM) for value in (rest, tail)],
+        *tables,
+    )
     return jnp.transpose(total, (1, 0, 2))
 
 

time: 57.3 us -> 56.9 us (level)
  Pallas kernels: 57.2 us -> 56.5 us
    pallas_call x1, Pallas kernels: 55 us -> 42.2 us  [local_part(): pl.pallas_call(functools.partial(kernel, unit, bounds), in_specs=[hbm] *...]
    pallas_call x1 -> x3, Pallas kernels: 2.2 us -> 14.4 us  [the longest x1 11.5 us: local_part(): pl.pallas_call(functools.partial(later_kernel, unit, written, later), in_...]
where the time goes in v5:
time: 56.9 us; the launch traced here: 56.6 us
  Pallas kernels  56.5 us (99%)
    pallas_call x1, Pallas kernels, local_part(): pl.pallas_call(functools.partial(kernel, unit, bounds), in_specs=[hbm] *...  42.2 us
    pallas_call x1, Pallas kernels, local_part(): pl.pallas_call(functools.partial(later_kernel, unit, written, later), in_...  11.5 us
    pallas_call x1, Pallas kernels, local_part(): pl.pallas_call(functools.partial(early_kernel, written * LANES), in_specs...  1.48 us
    pallas_call x1, Pallas kernels, local_part(): pl.pallas_call(finish_kernel, in_specs=[hbm] + [vmem] * 5, out_specs=hbm,...  1.36 us

profile of v5, /device:TPU:1, one launch (start us, length us, event | category | flops | bytes accessed | tf_op | source)
XLA Modules:
  0.0 56.6 jit_solution(11363381144222950090)
XLA Ops:
  0.0 42.2 %residual.1 = (f32[3,64,6144]{2,1,0:T(8,128)S(1)}, bf16[65,192,128]{2,1,0:T(8,128)(2,1)S(1)}, bf16[1,48,192,128]{3,2,1,0:T(8,128)(2,1)S(1)}, bf16[128,256]{1,0:T...) custom-call(s32[4,4,16]{2,1,0:T(4,128)} %bitcast.15, s32[4,48]{1,0:T(4,128)} %bitcast.16, ...), custom_call_target="tpu_custom_call" | custom-call | flops 2113929216 | bytes 20447232 | tf_op jit(solution)/shard_map/residual/pallas_call | solution.py:505
  42.2 1.5 %early.1 = (f32[3,64,6144]{2,1,0:T(8,128)}, f32[8,128]{1,0:T(8,128)S(1)}) custom-call(f32[3,64,6144]{2,1,0:T(8,128)S(1)} %get-tuple-element.15.total_ref), custom_call_target="tpu_custom_call" | custom-call | bytes 2555904 | tf_op jit(solution)/shard_map/early/pallas_call | solution.py:559
  43.7 11.5 %later.1 = (f32[3,64,2816]{2,1,0:T(8,128)S(1)}, bf16[2,2,192,128]{3,2,1,0:T(8,128)(2,1)S(1)}) custom-call(f32[8,128]{1,0:T(8,128)S(1)} %get-tuple-element.17._, f32[3,64,6144]{2,1,0:T(8,128)S(1)} %get-tuple-element.15.total_ref, bf16[65,192,128]{2,1,0:T(8,128)(2,1)S(1)} %get-tuple-element.18.pool_ref, ...), custom_call_target="tpu_custom_call" | custom-call | flops 415236096 | tf_op jit(solution)/shard_map/later/pallas_call | solution.py:572
  55.2 1.4 %finish.1 = f32[3,64,6144]{2,1,0:T(8,128)} custom-call(f32[3,64,6144]{2,1,0:T(8,128)} %get-tuple-element.16._, f32[3,64,2816]{2,1,0:T(8,128)S(1)} %get-tuple-element.23.rest_ref, bf16[2,2,192,128]{3,2,1,0:T(8,128)(2,1)S(1)} %get-tuple-element.24.tail_ref, bf16[128,256]{1,0:T(8,128)(2,1)S(1)} %get-tuple-element.20.synthesis_ref, ...), custom_call_target="tpu_custom_call", output_to_operand_aliasing={{}: (0, {})} | custom-call | flops 37748736 | bytes 2162688 | tf_op jit(solution)/shard_map/finish/pallas_call | solution.py:593

commit v6 on v5

--- a/solution.py
+++ b/solution.py
@@ -10,8 +10,8 @@
 
 LOG_TWO = 0.6931471805599453
 OFFSETS = (-2, -1, 1, 2)
-CUTS = (0, 2, 4, 14, 26, 36)
-LATER = (36, 42, 46, 48)
+CUTS = (0, 2, 4, 14, 26, 30)
+LATER = (30, 38, 42, 46, 48)
 TOTAL = 48
 LANES = 128
 VMEM_BYTES = 36 << 20
@@ -118,12 +118,8 @@
     shares = lax.axis_size("harm")
     me = lax.axis_index("harm")
     base = bounds[0]
-    barrier = pltpu.get_barrier_semaphore()
-    for by in range(1, shares):
-        pl.semaphore_signal(
-            barrier, inc=1, device_id={"harm": lax.rem(me + by, shares)}, device_id_type=MESH
-        )
-    pl.semaphore_wait(barrier, shares - 1)
+    late = lax.rem(lax.axis_index("node"), 2) == 1
+    final = bounds[-2]
 
     def exchange(low, high, by, recv):
         return pltpu.make_async_remote_copy(
@@ -136,9 +132,6 @@
         )
 
     pieces = list(zip(bounds[:-1], bounds[1:]))
-    for index, (low, high) in enumerate(pieces):
-        for by in range(1, shares):
-            exchange(low, high, by, index).start()
 
     def nonlinear(source_ref, shift, group, carry):
         ids = [group * unit + inner for inner in range(unit)]
@@ -160,28 +153,46 @@
             )
         return carry
 
-    lax.fori_loop(
-        written // unit, base // unit, functools.partial(nonlinear, before_ref, 0), 0
-    )
-    final = bounds[-2]
-    rest_ref[:, :, (final - written) * LANES :] = total_ref[:, :, final * LANES :]
-    tail_ref[0] = pool_ref[final:blocks]
-    for index, (low, high) in enumerate(pieces):
-        for by in range(1, shares):
-            exchange(low, high, by, index).wait_recv()
-        if high < blocks:
-            lax.fori_loop(
-                low // unit, high // unit, functools.partial(nonlinear, arrived_ref, base), 0
+    @pl.when(late)
+    def _():
+        barrier = pltpu.get_barrier_semaphore()
+        for by in range(1, shares):
+            pl.semaphore_signal(
+                barrier, inc=1, device_id={"harm": lax.rem(me + by, shares)}, device_id_type=MESH
             )
-    for by in range(1, shares):
-        tail_ref[by] = arrived_ref[by - 1, final - base :]
-    for by in range(1, shares):
-        exchange(base, blocks, by, 0).wait_send()
+        pl.semaphore_wait(barrier, shares - 1)
+        for index, (low, high) in enumerate(pieces):
+            for by in range(1, shares):
+                exchange(low, high, by, index).start()
+        lax.fori_loop(
+            written // unit, base // unit, functools.partial(nonlinear, before_ref, 0), 0
+        )
+        rest_ref[:, :, (final - written) * LANES :] = total_ref[:, :, final * LANES :]
+        tail_ref[0] = pool_ref[final:blocks]
+        for index, (low, high) in enumerate(pieces):
+            for by in range(1, shares):
+                exchange(low, high, by, index).wait_recv()
+            if high < blocks:
+                lax.fori_loop(
+                    low // unit, high // unit, functools.partial(nonlinear, arrived_ref, base), 0
+                )
+        for by in range(1, shares):
+            tail_ref[by] = arrived_ref[by - 1, final - base :]
+        for by in range(1, shares):
+            exchange(base, blocks, by, 0).wait_send()
+
+    @pl.when(jnp.logical_not(late))
+    def _():
+        rest_ref[...] = total_ref[:, :, written * LANES :]
+        tail_ref[0] = pool_ref[final:blocks]
+        for by in range(1, shares):
+            tail_ref[by] = before_ref[by - 1, final:blocks]
 
 
 def kernel(
     unit,
     bounds,
+    later,
     list_hbm,
     slot_hbm,
     x_hbm,
@@ -220,7 +231,7 @@
     blocks = nodes // LANES
     chunks = len(bounds) - 1
     loads = bounds[:3] + [blocks]
-    groups = bounds[:1] + bounds[3:]
+    groups = bounds[:1] + bounds[3:] + later[1:]
     count, slots = coupling_ref.shape[1], list_ref.shape[1]
     shares, devices = lax.axis_size("harm"), lax.axis_size("node")
     me, place = lax.axis_index("harm"), lax.axis_index("node")
@@ -366,11 +377,13 @@
         for slot in range(slots):
             packed_ref[direction, slot] = pool_ref[list_ref[direction, slot, place]]
     late = lax.rem(place, 2) == 1
-    kept = bounds[-2]
-
-    @pl.when(jnp.logical_not(late))
-    def _():
-        send(kept, bounds[-1])
+    soon = jnp.logical_not(late)
+    send(bounds[-2], bounds[-1])
+
+    @pl.when(soon)
+    def _():
+        for low, high in zip(later[:-1], later[1:]):
+            send(low, high)
 
     greet(group_sem)
 
@@ -450,20 +463,34 @@
             )
         return carry
 
-    last = len(groups) - 2
-    for group in range(last):
+    def receive(group):
         for by in range(1, shares):
             arrival(group, by).wait_recv()
+
+    def process(group):
         lax.fori_loop(groups[group] // unit, groups[group + 1] // unit, nonlinear, 0)
 
+    shared = groups.index(bounds[-1]) - 1
+    for group in range(shared):
+        receive(group)
+        process(group)
+    receive(shared)
+
+    @pl.when(soon)
+    def _():
+        process(shared)
+        for group in range(shared + 1, len(groups) - 1):
+            receive(group)
+            if group < len(groups) - 2:
+                process(group)
+        for by in range(1, shares):
+            exchange(0, blocks, by, 0).wait_send()
+
     @pl.when(late)
     def _():
-        send(kept, bounds[-1])
-
-    for by in range(1, shares):
-        arrival(last, by).wait_recv()
-    for by in range(1, shares):
-        exchange(0, bounds[-1], by, 0).wait_send()
+        for by in range(1, shares):
+            exchange(0, bounds[-1], by, 0).wait_send()
+
     for direction, offset in enumerate(OFFSETS):
 
         @pl.when(on_mesh(place + offset))
@@ -503,7 +530,7 @@
     hbm = pl.BlockSpec(memory_space=pltpu.HBM)
     bf16, f32 = jnp.bfloat16, jnp.float32
     held = pl.pallas_call(
-        functools.partial(kernel, unit, bounds),
+        functools.partial(kernel, unit, bounds, later),
         in_specs=[hbm] * 11,
         out_specs=[vmem] * 6,
         out_shape=[
@@ -524,7 +551,7 @@
             pltpu.SemaphoreType.DMA((3,)),
             pltpu.SemaphoreType.DMA((7,)),
             pltpu.SemaphoreType.DMA((shares - 1,)),
-            pltpu.SemaphoreType.DMA((shares - 1, len(bounds) - 3)),
+            pltpu.SemaphoreType.DMA((shares - 1, len(bounds) + len(later) - 4)),
             pltpu.SemaphoreType.DMA((directions,)),
             pltpu.SemaphoreType.DMA((directions,)),
         ]

time: 56.9 us -> 56.2 us (0.988)
    pallas_call x1, Pallas kernels: 42.2 us -> 35.3 us  [local_part(): pl.pallas_call(functools.partial(kernel, unit, bounds, later), in_specs=[...]
    pallas_call x1, Pallas kernels: 11.5 us -> 17.8 us  [local_part(): pl.pallas_call(functools.partial(later_kernel, unit, written, later), in_...]
where the time goes in v6:
time: 56.2 us; the launch traced here: 56 us
  Pallas kernels  56 us (100%)
    pallas_call x1, Pallas kernels, local_part(): pl.pallas_call(functools.partial(kernel, unit, bounds, later), in_specs=[...  35.3 us
    pallas_call x1, Pallas kernels, local_part(): pl.pallas_call(functools.partial(later_kernel, unit, written, later), in_...  17.8 us
    pallas_call x1, Pallas kernels, local_part(): pl.pallas_call(functools.partial(early_kernel, written * LANES), in_specs...  1.48 us
    pallas_call x1, Pallas kernels, local_part(): pl.pallas_call(finish_kernel, in_specs=[hbm] + [vmem] * 5, out_specs=hbm,...  1.36 us

profile of v6, /device:TPU:1, one launch (start us, length us, event | category | flops | bytes accessed | tf_op | source)
XLA Modules:
  0.0 56.0 jit_solution(1939946509433968759)
XLA Ops:
  0.0 35.3 %residual.1 = (f32[3,64,6144]{2,1,0:T(8,128)S(1)}, bf16[65,192,128]{2,1,0:T(8,128)(2,1)S(1)}, bf16[1,48,192,128]{3,2,1,0:T(8,128)(2,1)S(1)}, bf16[128,256]{1,0:T...) custom-call(s32[4,4,16]{2,1,0:T(4,128)} %bitcast.15, s32[4,48]{1,0:T(4,128)} %bitcast.16, ...), custom_call_target="tpu_custom_call" | custom-call | flops 2113929216 | bytes 20447232 | tf_op jit(solution)/shard_map/residual/pallas_call | solution.py:532
  35.3 1.5 %early.1 = (f32[3,64,6144]{2,1,0:T(8,128)}, f32[8,128]{1,0:T(8,128)S(1)}) custom-call(f32[3,64,6144]{2,1,0:T(8,128)S(1)} %get-tuple-element.15.total_ref), custom_call_target="tpu_custom_call" | custom-call | bytes 2555904 | tf_op jit(solution)/shard_map/early/pallas_call | solution.py:586
  36.8 17.8 %later.1 = (f32[3,64,2816]{2,1,0:T(8,128)S(1)}, bf16[2,2,192,128]{3,2,1,0:T(8,128)(2,1)S(1)}) custom-call(f32[8,128]{1,0:T(8,128)S(1)} %get-tuple-element.17._, f32[3,64,6144]{2,1,0:T(8,128)S(1)} %get-tuple-element.15.total_ref, bf16[65,192,128]{2,1,0:T(8,128)(2,1)S(1)} %get-tuple-element.18.pool_ref, ...), custom_call_target="tpu_custom_call" | custom-call | flops 415236096 | tf_op jit(solution)/shard_map/later/pallas_call | solution.py:599
  54.7 1.4 %finish.1 = f32[3,64,6144]{2,1,0:T(8,128)} custom-call(f32[3,64,6144]{2,1,0:T(8,128)} %get-tuple-element.16._, f32[3,64,2816]{2,1,0:T(8,128)S(1)} %get-tuple-element.23.rest_ref, bf16[2,2,192,128]{3,2,1,0:T(8,128)(2,1)S(1)} %get-tuple-element.24.tail_ref, bf16[128,256]{1,0:T(8,128)(2,1)S(1)} %get-tuple-element.20.synthesis_ref, ...), custom_call_target="tpu_custom_call", output_to_operand_aliasing={{}: (0, {})} | custom-call | flops 37748736 | bytes 2162688 | tf_op jit(solution)/shard_map/finish/pallas_call | solution.py:620

commit v7 on v6

--- a/solution.py
+++ b/solution.py
@@ -10,8 +10,8 @@
 
 LOG_TWO = 0.6931471805599453
 OFFSETS = (-2, -1, 1, 2)
-CUTS = (0, 2, 4, 14, 26, 30)
-LATER = (30, 38, 42, 46, 48)
+CUTS = (0, 2, 4, 14, 30, 34)
+LATER = (34, 40, 44, 46, 48)
 TOTAL = 48
 LANES = 128
 VMEM_BYTES = 36 << 20

time: 56.2 us -> 56 us (level)
    pallas_call x1, Pallas kernels: 17.8 us -> 13.4 us  [local_part(): pl.pallas_call(functools.partial(later_kernel, unit, written, later), in_...]
    pallas_call x1, Pallas kernels: 35.3 us -> 39.6 us  [local_part(): pl.pallas_call(functools.partial(kernel, unit, bounds, later), in_specs=[...]
where the time goes in v7:
time: 56 us; the launch traced here: 55.9 us
  Pallas kernels  55.9 us (100%)
    pallas_call x1, Pallas kernels, local_part(): pl.pallas_call(functools.partial(kernel, unit, bounds, later), in_specs=[...  39.6 us
    pallas_call x1, Pallas kernels, local_part(): pl.pallas_call(functools.partial(later_kernel, unit, written, later), in_...  13.4 us
    pallas_call x1, Pallas kernels, local_part(): pl.pallas_call(functools.partial(early_kernel, written * LANES), in_specs...  1.61 us
    pallas_call x1, Pallas kernels, local_part(): pl.pallas_call(finish_kernel, in_specs=[hbm] + [vmem] * 5, out_specs=hbm,...  1.23 us

profile of v7, /device:TPU:1, one launch (start us, length us, event | category | flops | bytes accessed | tf_op | source)
XLA Modules:
  0.0 55.9 jit_solution(16030027020649739468)
XLA Ops:
  0.0 39.6 %residual.1 = (f32[3,64,6144]{2,1,0:T(8,128)S(1)}, bf16[65,192,128]{2,1,0:T(8,128)(2,1)S(1)}, bf16[1,48,192,128]{3,2,1,0:T(8,128)(2,1)S(1)}, bf16[128,256]{1,0:T...) custom-call(s32[4,4,16]{2,1,0:T(4,128)} %bitcast.15, s32[4,48]{1,0:T(4,128)} %bitcast.16, ...), custom_call_target="tpu_custom_call" | custom-call | flops 2113929216 | bytes 20447232 | tf_op jit(solution)/shard_map/residual/pallas_call | solution.py:532
  39.6 1.6 %early.1 = (f32[3,64,6144]{2,1,0:T(8,128)}, f32[8,128]{1,0:T(8,128)S(1)}) custom-call(f32[3,64,6144]{2,1,0:T(8,128)S(1)} %get-tuple-element.15.total_ref), custom_call_target="tpu_custom_call" | custom-call | bytes 2949120 | tf_op jit(solution)/shard_map/early/pallas_call | solution.py:586
  41.2 13.4 %later.1 = (f32[3,64,2304]{2,1,0:T(8,128)S(1)}, bf16[2,2,192,128]{3,2,1,0:T(8,128)(2,1)S(1)}) custom-call(f32[8,128]{1,0:T(8,128)S(1)} %get-tuple-element.17._, f32[3,64,6144]{2,1,0:T(8,128)S(1)} %get-tuple-element.15.total_ref, bf16[65,192,128]{2,1,0:T(8,128)(2,1)S(1)} %get-tuple-element.18.pool_ref, ...), custom_call_target="tpu_custom_call" | custom-call | flops 339738624 | tf_op jit(solution)/shard_map/later/pallas_call | solution.py:599
  54.6 1.2 %finish.1 = f32[3,64,6144]{2,1,0:T(8,128)} custom-call(f32[3,64,6144]{2,1,0:T(8,128)} %get-tuple-element.16._, f32[3,64,2304]{2,1,0:T(8,128)S(1)} %get-tuple-element.23.rest_ref, bf16[2,2,192,128]{3,2,1,0:T(8,128)(2,1)S(1)} %get-tuple-element.24.tail_ref, bf16[128,256]{1,0:T(8,128)(2,1)S(1)} %get-tuple-element.20.synthesis_ref, ...), custom_call_target="tpu_custom_call", output_to_operand_aliasing={{}: (0, {})} | custom-call | flops 37748736 | bytes 1769472 | tf_op jit(solution)/shard_map/finish/pallas_call | solution.py:620
